TPU v7x, 32 devices: a whole 2x2x4 slice. The times are simulated.
32 devices in a mesh: row: 4 (over y, x), col: 8 (over z, core).
Axes of the slice: x: 2, y: 2, z: 4, core: 2. Of those that a mesh axis runs over, the one named last changes fastest.
Arguments:
- pair_rep: bfloat16 [96, 96, 128], P('row', 'col'), may hold values from -6 to 6
- pair_mask: int32 [96, 96], P('row', 'col'), may hold values 0 or 1
- proj_weight: bfloat16 [2, 5, 128, 128], replicated, may hold values from -0.5 to 0.5
- out_weight: bfloat16 [2, 128, 128], replicated, may hold values from -0.5 to 0.5
- norm_gain: float32 [2, 2, 128], replicated, may hold values from 0.25 to 1.75
- norm_bias: float32 [2, 2, 128], replicated, may hold values from -1.5 to 1.5
Outputs:
- pair_out: bfloat16 [96, 96, 128], P('row', 'col')
Inputs may be any that keep to these rules, and one draw needn't show every extreme that they name: pair_mask holds only 0 and 1.
All inputs are finite; a program needn't handle non-finite values.
Results may differ from a plain program's by a relative error of at most 0.0095.
Values may be sent and summed in bfloat16 or wider, within the bound.
A program may use at most 64 MiB of HBM per device.

v0:
```python
import jax
import jax.numpy as jnp
from jax import lax
from jax.sharding import PartitionSpec as P

epsilon = 1e-05


def scattered(term, extent, axis):
    whole = term(jnp.int32(0), extent * lax.axis_size(axis))
    return lax.psum_scatter(whole, axis, scatter_dimension=0, tiled=True)


def layer_norm(values, gain_vec, bias_vec):
    average = jnp.mean(values, axis=-1, keepdims=True)
    centred = values - average
    variance = jnp.mean(centred * centred, axis=-1, keepdims=True)
    return centred * lax.rsqrt(variance + epsilon) * gain_vec + bias_vec


def projections(pair_rep, mask_float, proj_weight, norm_gain, norm_bias, layer_no):
    channels = pair_rep.shape[2]
    normed = layer_norm(
        pair_rep.astype(jnp.float32), norm_gain[layer_no, 0], norm_bias[layer_no, 0]
    ).astype(jnp.bfloat16)
    flattened = normed.reshape(-1, channels)
    products = [
        jnp.dot(
            flattened, proj_weight[layer_no, which], preferred_element_type=jnp.float32
        ).reshape(pair_rep.shape)
        for which in range(5)
    ]
    left_side = (jax.nn.sigmoid(products[0]) * products[1] * mask_float).astype(jnp.bfloat16)
    right_side = (jax.nn.sigmoid(products[2]) * products[3] * mask_float).astype(jnp.bfloat16)
    gate_value = jax.nn.sigmoid(products[4])
    return (left_side, right_side, gate_value)


def finish(pair_rep, triangle, gate_value, out_weight, norm_gain, norm_bias, layer_no):
    channels = pair_rep.shape[2]
    normed = layer_norm(triangle, norm_gain[layer_no, 1], norm_bias[layer_no, 1]).astype(
        jnp.bfloat16
    )
    projected = jnp.dot(
        normed.reshape(-1, channels), out_weight[layer_no], preferred_element_type=jnp.float32
    ).reshape(pair_rep.shape)
    return (pair_rep.astype(jnp.float32) + gate_value * projected).astype(jnp.bfloat16)


def shards(pair_rep, pair_mask, proj_weight, out_weight, norm_gain, norm_bias):
    rows_dev, cols_dev, channels = pair_rep.shape
    mask_float = pair_mask.astype(jnp.float32)[..., None]
    left_side, right_side, gate_value = projections(
        pair_rep, mask_float, proj_weight, norm_gain, norm_bias, 0
    )
    right_all = lax.all_gather(right_side, "row", axis=0, tiled=True)

    def outgoing_term(first_idx, how_many):
        sliced = lax.dynamic_slice_in_dim(right_all, first_idx, how_many, 0)
        return jnp.einsum("jkc,ikc->jic", sliced, left_side, preferred_element_type=jnp.float32)

    triangle = scattered(outgoing_term, cols_dev, "col")
    triangle = jnp.transpose(triangle, (1, 0, 2))
    pair_rep = finish(pair_rep, triangle, gate_value, out_weight, norm_gain, norm_bias, 0)
    left_side, right_side, gate_value = projections(
        pair_rep, mask_float, proj_weight, norm_gain, norm_bias, 1
    )
    left_all = lax.all_gather(left_side, "col", axis=1, tiled=True)

    def incoming_term(first_idx, how_many):
        sliced = lax.dynamic_slice_in_dim(left_all, first_idx, how_many, 1)
        return jnp.einsum("kic,kjc->ijc", sliced, right_side, preferred_element_type=jnp.float32)

    triangle = scattered(incoming_term, rows_dev, "row")
    pair_rep = finish(pair_rep, triangle, gate_value, out_weight, norm_gain, norm_bias, 1)
    return pair_rep


def solution(mesh):
    in_specs = (P("row", "col", None), P("row", "col"), P(), P(), P(), P())
    out_specs = P("row", "col", None)
    return jax.shard_map(shards, mesh=mesh, in_specs=in_specs, out_specs=out_specs, check_vma=False)
```

profile of v0, /device:TPU:0, one launch (start us, length us, event | category | flops | bytes accessed | tf_op | source)
XLA Modules:
  0.0 136.7 jit_solution(15166773543570996231)
XLA Ops:
  6.5 1.0 convert_reduce_fusion
  7.5 1.1 fusion.39
  8.6 0.8 slice_bitcast_fusion
  9.4 1.2 fusion.60
  10.6 1.2 fusion.57
  11.8 0.7 convert_element_type.43
  12.5 1.2 fusion.34
  13.7 1.2 fusion.33
  14.8 11.0 %all_gather.6 = bf16[96,12,128]{2,0,1:T(8,128)(2,1)S(1)} all-gather(bf16[24,12,128]{2,0,1:T(8,128)(2,1)S(1)} %fusion.33), channel_id=1, replica_groups=mesh['row'=4,'col'=8] {'row'}, dimensions={0}, use_global_device_ids=true | all-gather | bytes 368640 | tf_op jit(solution)/shard_map/all_gather | solution.py:56
  25.9 0.4 copy.44
  26.3 0.4 copy.43
  26.8 0.6 convolution_bitcast_fusion
  27.4 1.6 %copy.45 = f32[96,24,128]{2,1,0:T(8,128)} copy(f32[96,24,128]{0,1,2:T(8,128)S(1)} %convolution_bitcast_fusion) | data formatting | bytes 2359296 | tf_op jit(solution)/shard_map/jkc,ikc->jic/transpose | solution.py:60
  29.0 33.2 %reduce-scatter.3.cloned.1.call-done = f32[12,24,128]{2,1,0:T(8,128)} async-done(((f32[96,24,128]{2,1,0:T(8,128)}), f32[12,24,128]{2,1,0:T(8,128)}) %reduce-scatter.3.cloned.1.call-update) | async-done | bytes 147472 | tf_op jit(solution)/shard_map/reduce_scatter | solution.py:11
  62.3 1.0 bitcast_reduce_fusion
  63.3 1.1 multiply_reduce_fusion.2
  64.4 1.2 fusion.43
  65.6 1.1 fusion.83
  67.1 0.9 fusion.50
  68.1 0.9 fusion.53
  69.0 1.0 fusion.30
  70.0 1.0 fusion.31
  70.9 1.2 copy.50
  72.1 15.8 %all_gather.7 = bf16[24,96,128]{2,0,1:T(8,128)(2,1)} all-gather(bf16[24,12,128]{2,0,1:T(8,128)(2,1)S(1)} %fusion.30), channel_id=1, replica_groups=mesh['row'=4,'col'=8] {'col'}, dimensions={1}, use_global_device_ids=true | all-gather | bytes 663552 | tf_op jit(solution)/shard_map/all_gather | solution.py:68
  88.0 5.2 %copy.51 = bf16[24,96,128]{0,1,2:T(8,128)(2,1)S(1)} copy(bf16[24,96,128]{2,0,1:T(8,128)(2,1)} %all_gather.7) | data formatting | bytes 1179648 | tf_op jit(solution)/shard_map/all_gather | solution.py:68
  93.2 3.8 %convolution_bitcast_fusion.1 = f32[96,12,128]{0,1,2:T(8,128)} fusion(bf16[24,12,128]{0,1,2:T(8,128)(2,1)} %copy.50, bf16[24,96,128]{0,1,2:T(8,128)(2,1)S(1)} %copy.51), kind=kOutput, calls=%fused_computation.1 | convolution fusion | flops 7077888 | bytes 1253376 | tf_op jit(solution)/shard_map/kic,kjc->ijc/dot_general | solution.py:72
  97.0 2.7 %copy.52 = f32[96,12,128]{2,1,0:T(8,128)} copy(f32[96,12,128]{0,1,2:T(8,128)} %convolution_bitcast_fusion.1) | data formatting | bytes 1179648 | tf_op jit(solution)/shard_map/kic,kjc->ijc/transpose | solution.py:72
  99.7 24.7 %reduce-scatter.5.cloned.1.call-done = f32[24,12,128]{2,1,0:T(8,128)} async-done(((f32[96,12,128]{2,1,0:T(8,128)}), f32[24,12,128]{2,1,0:T(8,128)}) %reduce-scatter.5.cloned.1.call-update) | async-done | bytes 147472 | tf_op jit(solution)/shard_map/reduce_scatter | solution.py:11
  124.4 1.0 reduce_sum.78
  125.7 1.1 multiply_reduce_fusion
  127.0 1.1 add_convert_fusion
  128.3 1.6 %fusion.32 = bf16[24,12,128]{2,0,1:T(8,128)(2,1)} fusion(f32[24,12,128]{2,0,1:T(8,128)S(1)} %get-tuple-element.14, f32[24,12,128]{2,0,1:T(8,128)S(1)} %fusion.44, bf16[24,12,128]{2,0,1:T(8,128)(2,1)S(1)} %add_convert_fusion.1, bf16[2,5,128,128]{3,2,1,0:T(8,128)(2,1)} %param.8), kind=kOutput, calls=%fused_computation.40 | convolution fusion | flops 9658368 | bytes 475136 | tf_op jit(solution)/shard_map/dot_general | solution.py:28
  (23 shorter events, 1.0 us)
Async XLA Ops:
  6.5 55.7 %reduce-scatter.3.cloned.1.call-start = ((), (), s32[]{:S(2)}) async-start(), calls=%async_computation.2 | async-start | bytes 1327104 | tf_op jit(solution)/shard_map/reduce_scatter | solution.py:11
  26.7 37.7 %copy-start.1 = (bf16[2,128,128]{2,1,0:T(8,128)(2,1)S(1)}, bf16[2,128,128]{2,1,0:T(8,128)(2,1)}, u32[]{:S(2)}) copy-start(bf16[2,128,128]{2,1,0:T(8,128)(2,1)} %param.9) | copy-start | bytes 196612
  26.8 38.9 %copy-start = (bf16[24,12,128]{2,0,1:T(8,128)(2,1)S(1)}, bf16[24,12,128]{2,0,1:T(8,128)(2,1)}, u32[]{:S(2)}) copy-start(bf16[24,12,128]{2,0,1:T(8,128)(2,1)} %param.6) | copy-start | bytes 221188
  29.0 95.4 %reduce-scatter.5.cloned.1.call-start = ((), (), s32[]{:S(2)}) async-start(), calls=%async_computation.3 | async-start | bytes 983040 | tf_op jit(solution)/shard_map/reduce_scatter | solution.py:11
Sparse Core Ops, SparseCore 0:
  29.1 33.0 reduce-scatter.2
  99.8 24.5 reduce-scatter.4
where the time goes:
time: 138 us; the launch traced here: 137 us
  waiting for transfers between devices  58 us (42%)
  blocking collectives  26.8 us (19%)
  matrix products  16.9 us (12%)
  between operations  13.6 us (10%)
  local copies, waits for them, and re-layouts  12.7 us (9%)
  other arithmetic  8.57 us (6%)
    reduce_scatter x2, waiting for transfers between devices, scattered(): return lax.psum_scatter(whole, axis, scatter_dimension=0, tiled=True)  58 us
    all_gather x1, blocking collectives, shards(): left_all = lax.all_gather(left_side, 'col', axis=1, tiled=True)  15.8 us
    dot_general x10, matrix products, projections(): jnp.dot(flattened, proj_weight[layer_no, which], preferred_element_type=j...  11.2 us
    all_gather x1, blocking collectives, shards(): right_all = lax.all_gather(right_side, 'row', axis=0, tiled=True)  11 us
    all_gather x1, local copies, waits for them, and re-layouts, shards(): left_all = lax.all_gather(left_side, 'col', axis=1, tiled=True)  5.24 us
    dot_general x1, matrix products, incoming_term(): jnp.einsum('kic,kjc->ijc', sliced, right_side, preferred_element_type=jnp...  3.77 us
    reduce_sum x4, other arithmetic, layer_norm(): variance = jnp.mean(centred * centred, axis=-1, keepdims=True)  3.5 us
    reduce_sum x3, other arithmetic, layer_norm(): average = jnp.mean(values, axis=-1, keepdims=True)  3.06 us
  transfers between devices with their start and end apart: 2, of which 2 were waited for; matrix products, arithmetic and copies ran while one was open for 0% of the time, Pallas kernels for 0%

commit v1 on v0

--- a/solution.py
+++ b/solution.py
@@ -1,6 +1,8 @@
 import jax
 import jax.numpy as jnp
 from jax import lax
+from jax.experimental import pallas as pl
+from jax.experimental.pallas import tpu as pltpu
 from jax.sharding import PartitionSpec as P
 
 epsilon = 1e-05
@@ -76,7 +78,246 @@
     return pair_rep
 
 
+def layer_norm_rows(values, gain_vec, bias_vec):
+    average = jnp.mean(values, axis=-1, keepdims=True)
+    centred = values - average
+    variance = jnp.mean(centred * centred, axis=-1, keepdims=True)
+    return centred * lax.rsqrt(variance + epsilon) * gain_vec + bias_vec
+
+
+def swapped(arrays, wanted, width, lane):
+    groups = lane.shape[1] // width
+    steps = []
+    m = groups // 2
+    while m:
+        steps.append(m)
+        m //= 2
+    memo = {}
+
+    def level(n, a):
+        if n == 0:
+            return arrays.get(a)
+        if (n, a) not in memo:
+            m = steps[n - 1]
+            low, high = level(n - 1, a & ~m), level(n - 1, a | m)
+            if a & m:
+                moved = None if low is None else pltpu.roll(low, (groups - m) * width, 1)
+                kept, other = high, moved
+                pick_kept = (lane // width) & m != 0
+            else:
+                moved = None if high is None else pltpu.roll(high, m * width, 1)
+                kept, other = low, moved
+                pick_kept = (lane // width) & m == 0
+            if kept is None:
+                memo[n, a] = other
+            elif other is None:
+                memo[n, a] = kept
+            else:
+                memo[n, a] = jnp.where(pick_kept, kept, other)
+        return memo[n, a]
+
+    return {a: level(len(steps), a) for a in wanted}
+
+
+def make_kernel(n_row, n_col, rows, cols, channels):
+    n_dev = n_row * n_col
+    width = channels // n_dev
+    span = cols * width
+    n_i, n_j = n_row * rows, n_col * cols
+    pitch = -(-cols // 8) * 8
+    bf16, f32 = jnp.bfloat16, jnp.float32
+
+    def kernel(
+        pair_ref, mask_ref, proj_ref, out_w_ref, gain_ref, bias_ref, out_ref,
+        flat, expanded, square, outbox, inbox, back_out, back_in,
+        send_sem, recv_sem,
+    ):
+        me_row, me_col = lax.axis_index("row"), lax.axis_index("col")
+        me = me_row * n_col + me_col
+        barrier = pltpu.get_barrier_semaphore()
+
+        def place(offset):
+            other = lax.rem(me + offset, n_dev)
+            return other, (other // n_col, lax.rem(other, n_col))
+
+        def greet(offset, carry):
+            pl.semaphore_signal(
+                barrier, inc=1, device_id=place(offset)[1],
+                device_id_type=pl.DeviceIdType.MESH,
+            )
+            return carry
+
+        lax.fori_loop(1, n_dev, greet, 0)
+
+        def copy(source, target, phase, offset):
+            other, where = place(offset)
+            return pltpu.make_async_remote_copy(
+                src_ref=source.at[other], dst_ref=target.at[me],
+                send_sem=send_sem.at[phase, other], recv_sem=recv_sem.at[phase, me],
+                device_id=where, device_id_type=pl.DeviceIdType.MESH,
+            )
+
+        def arrival(source, target, phase, offset):
+            other, where = place(offset)
+            return pltpu.make_async_remote_copy(
+                src_ref=source.at[other], dst_ref=target.at[other],
+                send_sem=send_sem.at[phase, other], recv_sem=recv_sem.at[phase, other],
+                device_id=where, device_id_type=pl.DeviceIdType.MESH,
+            )
+
+        def exchange(source, target, phase):
+            target[pl.ds(me, 1)] = source[pl.ds(me, 1)]
+
+            def send(offset, carry):
+                copy(source, target, phase, offset).start()
+                return carry
+
+            def receive(offset, carry):
+                arrival(source, target, phase, offset).wait_recv()
+                return carry
+
+            lax.fori_loop(1, n_dev, send, 0)
+            lax.fori_loop(1, n_dev, receive, 0)
+
+        lane = lax.broadcasted_iota(jnp.int32, (rows, channels), 1)
+        tall_lane = lax.broadcasted_iota(jnp.int32, (n_i, channels), 1)
+        mask_float = mask_ref[...].astype(f32)
+
+        for i in range(rows):
+            flat[pitch * i : pitch * i + cols, :] = pair_ref[i].astype(f32)
+        z = jnp.concatenate(
+            [flat[pl.ds(j, rows, stride=pitch), :] for j in range(cols)], axis=0
+        )
+
+        for update in range(2):
+            normed = layer_norm_rows(
+                z, gain_ref[update, 0:1, :], bias_ref[update, 0:1, :]
+            ).astype(bf16)
+            products = [
+                jnp.dot(normed, proj_ref[update, which], preferred_element_type=f32)
+                for which in range(5)
+            ]
+            sides = {}
+            for side in range(2):
+                values = jax.nn.sigmoid(products[2 * side]) * products[2 * side + 1]
+                for k in range(cols):
+                    sides[side * cols + k] = (
+                        values[k * rows : (k + 1) * rows, :] * mask_float[:, k : k + 1]
+                    )
+            gate_value = jax.nn.sigmoid(products[4])
+            parcels = swapped(sides, range(n_dev), width, lane)
+            for d in range(n_dev):
+                outbox[update, d] = parcels[d].astype(bf16)
+            if update == 0:
+                pl.semaphore_wait(barrier, n_dev - 1)
+            exchange(outbox.at[update], inbox.at[update], 2 * update)
+
+            blocks = [
+                jnp.concatenate(
+                    [inbox[update, r * n_col + c].astype(f32) for r in range(n_row)], axis=0
+                )
+                for c in range(n_col)
+            ]
+            if update == 0:
+                for c in range(n_col):
+                    moved = pltpu.roll(blocks[c], channels - span, 1)
+                    for q in range(width):
+                        expanded[c, pl.ds(q, n_i, stride=width), :] = jnp.where(
+                            (tall_lane < span) & (tall_lane % width == q), moved, 0.0
+                        )
+                triangle = lax.dot_general(
+                    jnp.concatenate(blocks, axis=1).astype(bf16),
+                    jnp.concatenate([expanded[c] for c in range(n_col)], axis=1).astype(bf16),
+                    (((1,), (1,)), ((), ())),
+                    preferred_element_type=f32,
+                )
+            else:
+                lefts = jnp.concatenate([b[:, :span] for b in blocks], axis=1)
+                rights = jnp.concatenate([b[:, span : 2 * span] for b in blocks], axis=1)
+                whole = jnp.dot(
+                    lefts.T.astype(bf16), rights.astype(bf16), preferred_element_type=f32
+                )
+                pieces = []
+                for g in range(n_j * width // channels):
+                    square[g] = whole[:, g * channels : (g + 1) * channels]
+                    piece = square[g, pl.ds(0, n_i, stride=width), :]
+                    for q in range(1, width):
+                        piece = jnp.where(
+                            tall_lane % width == q,
+                            square[g, pl.ds(q, n_i, stride=width), :],
+                            piece,
+                        )
+                    pieces.append(piece)
+                triangle = jnp.concatenate(pieces, axis=1)
+            for c in range(n_col):
+                part = triangle[:, c * span : (c + 1) * span]
+                for r in range(n_row):
+                    back_out[update, r * n_col + c, :, :span] = (
+                        part[r * rows : (r + 1) * rows, :].astype(bf16)
+                    )
+            exchange(back_out.at[update], back_in.at[update], 2 * update + 1)
+
+            sums = swapped(
+                {d: back_in[update, d].astype(f32) for d in range(n_dev)},
+                range(cols), width, lane,
+            )
+            own = jnp.concatenate([sums[j] for j in range(cols)], axis=0)
+            tnorm = layer_norm_rows(
+                own, gain_ref[update, 1:2, :], bias_ref[update, 1:2, :]
+            ).astype(bf16)
+            projected = jnp.dot(tnorm, out_w_ref[update], preferred_element_type=f32)
+            z = (z + gate_value * projected).astype(bf16).astype(f32)
+
+        for j in range(cols):
+            flat[pl.ds(j, rows, stride=pitch), :] = z[j * rows : (j + 1) * rows, :]
+        for i in range(rows):
+            out_ref[i] = flat[pitch * i : pitch * i + cols, :].astype(bf16)
+
+        def sent(offset, carry):
+            for update in range(2):
+                copy(outbox.at[update], inbox.at[update], 2 * update, offset).wait_send()
+                copy(back_out.at[update], back_in.at[update], 2 * update + 1, offset).wait_send()
+            return carry
+
+        lax.fori_loop(1, n_dev, sent, 0)
+
+    parcel = pltpu.VMEM((2, n_dev, rows, channels), bf16)
+    return pl.pallas_call(
+        kernel,
+        out_shape=jax.ShapeDtypeStruct((rows, cols, channels), bf16),
+        in_specs=[pl.BlockSpec(memory_space=pltpu.VMEM)] * 6,
+        out_specs=pl.BlockSpec(memory_space=pltpu.VMEM),
+        scratch_shapes=[
+            pltpu.VMEM((rows * pitch, channels), f32),
+            pltpu.VMEM((n_col, n_j * width, channels), f32),
+            pltpu.VMEM((n_j * width // channels, n_i * width, channels), f32),
+            parcel, parcel, parcel, parcel,
+            pltpu.SemaphoreType.DMA((4, n_dev)),
+            pltpu.SemaphoreType.DMA((4, n_dev)),
+        ],
+        compiler_params=pltpu.CompilerParams(collective_id=0, has_side_effects=True),
+    )
+
+
 def solution(mesh):
+    n_row, n_col = mesh.shape["row"], mesh.shape["col"]
+    n_dev = n_row * n_col
+
+    def local(pair_rep, *others):
+        rows, cols, channels = pair_rep.shape
+        by_channel = (
+            channels == 128
+            and channels % n_dev == 0
+            and n_dev & (n_dev - 1) == 0
+            and 2 * cols <= n_dev
+            and rows % 8 == 0
+            and n_row * rows == n_col * cols
+            and n_col * cols * (channels // n_dev) % channels == 0
+        )
+        if by_channel:
+            return make_kernel(n_row, n_col, rows, cols, channels)(pair_rep, *others)
+        return shards(pair_rep, *others)
+
     in_specs = (P("row", "col", None), P("row", "col"), P(), P(), P(), P())
     out_specs = P("row", "col", None)
-    return jax.shard_map(shards, mesh=mesh, in_specs=in_specs, out_specs=out_specs, check_vma=False)
+    return jax.shard_map(local, mesh=mesh, in_specs=in_specs, out_specs=out_specs, check_vma=False)

time: 138 us -> 45.7 us (0.33)
  waiting for transfers between devices: 58 us -> 0 us
  Pallas kernels: 0 us -> 41 us
  blocking collectives: 26.8 us -> 0 us
  matrix products: 16.9 us -> 0 us
  between operations: 13.6 us -> 0.01 us
  other arithmetic: 8.57 us -> 0 us
  local copies, waits for them, and re-layouts: 12.7 us -> 4.44 us
    reduce_scatter x2 -> x0, waiting for transfers between devices: 58 us -> none  [scattered(): return lax.psum_scatter(whole, axis, scatter_dimension=0, tiled=True)]
    pallas_call x0 -> x1, Pallas kernels: none -> 41 us  [local(): return make_kernel(n_row, n_col, rows, cols, channels)(pair_rep, *others)]
    all_gather x2 -> x0, blocking collectives: 26.8 us -> none  [the longest x1 15.8 us: shards(): left_all = lax.all_gather(left_side, 'col', axis=1, tiled=True)]
    dot_general x14 -> x0, matrix products: 16.9 us -> none  [the longest x10 11.2 us: projections(): jnp.dot(flattened, proj_weight[layer_no, which], preferred_element_type=j...]
    reduce_sum x7 -> x0, other arithmetic: 6.56 us -> none  [the longest x4 3.5 us: layer_norm(): variance = jnp.mean(centred * centred, axis=-1, keepdims=True)]
    all_gather x2 -> x0, local copies, waits for them, and re-layouts: 5.67 us -> none  [the longest x1 5.24 us: shards(): left_all = lax.all_gather(left_side, 'col', axis=1, tiled=True)]
    transpose x2 -> x0, local copies, waits for them, and re-layouts: 4.25 us -> none  [the longest x1 2.69 us: incoming_term(): jnp.einsum('kic,kjc->ijc', sliced, right_side, preferred_element_type=jnp...]
    unnamed x4 -> x2, local copies, waits for them, and re-layouts: 0.01 us -> 2.89 us
  transfers between devices with their start and end apart: 2 -> 0, of which waited for: 2 -> 0; matrix products, arithmetic and copies ran while one was open for 0% -> 0% of each run, Pallas kernels for 0% -> 0%
where the time goes in v1:
time: 45.7 us; the launch traced here: 45.4 us
  Pallas kernels  41 us (90%)
  local copies, waits for them, and re-layouts  4.44 us (10%)
    pallas_call x1, Pallas kernels, local(): return make_kernel(n_row, n_col, rows, cols, channels)(pair_rep, *others)  41 us
    unnamed x2, local copies, waits for them, and re-layouts  2.89 us
    pallas_call x1, local copies, waits for them, and re-layouts, local(): return make_kernel(n_row, n_col, rows, cols, channels)(pair_rep, *others)  1.55 us

profile of v1, /device:TPU:0, one launch (start us, length us, event | category | flops | bytes accessed | tf_op | source)
XLA Modules:
  0.0 45.4 jit_solution(8152467721145156124)
XLA Ops:
  0.0 1.4 %copy.8.mask_ref = s32[24,12]{1,0:T(8,128)} copy(s32[24,12]{0,1:T(8,128)} %param.7) | data formatting | bytes 2304 | tf_op args[1]
  1.4 1.5 %copy.7.pair_ref = bf16[24,12,128]{2,1,0:T(8,128)(2,1)} copy(bf16[24,12,128]{2,0,1:T(8,128)(2,1)} %param.6) | data formatting | bytes 147456 | tf_op args[0]
  2.9 41.0 %shard_map.64 = bf16[24,12,128]{2,1,0:T(8,128)(2,1)} custom-call(bf16[24,12,128]{2,1,0:T(8,128)(2,1)} %copy.7.pair_ref, s32[24,12]{1,0:T(8,128)} %copy.8.mask_ref, bf16[2,5,128,128]{3,2,1,0:T(8,128)(2,1)} %proj_ref.1, bf16[2,128,128]{2,1,0:T(8,128)(2,1)} %out_w_ref.1, f32[2,2,128]{2,1,0:T(2,128)} %gain_ref.1, f32[2,2,128]{2,1,0:T(2,128)} %bias_ref.1), custom_call_target="tpu_custom_call" | custom-call | tf_op jit(solution)/shard_map/pallas_call | solution.py:318
  43.9 1.5 %copy.9 = bf16[24,12,128]{2,0,1:T(8,128)(2,1)} copy(bf16[24,12,128]{2,1,0:T(8,128)(2,1)} %shard_map.64) | data formatting | bytes 147456 | tf_op jit(solution)/shard_map/pallas_call | solution.py:318

commit v2 on v1

--- a/solution.py
+++ b/solution.py
@@ -124,12 +124,12 @@
     width = channels // n_dev
     span = cols * width
     n_i, n_j = n_row * rows, n_col * cols
-    pitch = -(-cols // 8) * 8
+    upper = -(-rows // 16) * 8
     bf16, f32 = jnp.bfloat16, jnp.float32
 
     def kernel(
         pair_ref, mask_ref, proj_ref, out_w_ref, gain_ref, bias_ref, out_ref,
-        flat, expanded, square, outbox, inbox, back_out, back_in,
+        expanded, square, outbox, inbox, back_out, back_in,
         send_sem, recv_sem,
     ):
         me_row, me_col = lax.axis_index("row"), lax.axis_index("col")
@@ -181,13 +181,9 @@
 
         lane = lax.broadcasted_iota(jnp.int32, (rows, channels), 1)
         tall_lane = lax.broadcasted_iota(jnp.int32, (n_i, channels), 1)
-        mask_float = mask_ref[...].astype(f32)
-
-        for i in range(rows):
-            flat[pitch * i : pitch * i + cols, :] = pair_ref[i].astype(f32)
-        z = jnp.concatenate(
-            [flat[pl.ds(j, rows, stride=pitch), :] for j in range(cols)], axis=0
-        )
+        mask_float = mask_ref[...].astype(f32).T
+
+        z = jnp.concatenate([pair_ref[j].astype(f32) for j in range(cols)], axis=0)
 
         for update in range(2):
             normed = layer_norm_rows(
@@ -252,13 +248,19 @@
             for c in range(n_col):
                 part = triangle[:, c * span : (c + 1) * span]
                 for r in range(n_row):
-                    back_out[update, r * n_col + c, :, :span] = (
-                        part[r * rows : (r + 1) * rows, :].astype(bf16)
-                    )
+                    mine = part[r * rows : (r + 1) * rows, :].astype(bf16)
+                    back_out[update, r * n_col + c, :, :span] = mine[:upper, :]
+                    back_out[update, r * n_col + c, : rows - upper, span : 2 * span] = mine[upper:, :]
             exchange(back_out.at[update], back_in.at[update], 2 * update + 1)
 
+            arrived = {}
+            for d in range(n_dev):
+                packed = back_in[update, d].astype(f32)
+                arrived[d] = jnp.concatenate(
+                    [packed, pltpu.roll(packed[: rows - upper], channels - span, 1)], axis=0
+                )
             sums = swapped(
-                {d: back_in[update, d].astype(f32) for d in range(n_dev)},
+                arrived,
                 range(cols), width, lane,
             )
             own = jnp.concatenate([sums[j] for j in range(cols)], axis=0)
@@ -269,9 +271,7 @@
             z = (z + gate_value * projected).astype(bf16).astype(f32)
 
         for j in range(cols):
-            flat[pl.ds(j, rows, stride=pitch), :] = z[j * rows : (j + 1) * rows, :]
-        for i in range(rows):
-            out_ref[i] = flat[pitch * i : pitch * i + cols, :].astype(bf16)
+            out_ref[j] = z[j * rows : (j + 1) * rows, :].astype(bf16)
 
         def sent(offset, carry):
             for update in range(2):
@@ -282,16 +282,16 @@
         lax.fori_loop(1, n_dev, sent, 0)
 
     parcel = pltpu.VMEM((2, n_dev, rows, channels), bf16)
+    back = pltpu.VMEM((2, n_dev, upper, channels), bf16)
     return pl.pallas_call(
         kernel,
-        out_shape=jax.ShapeDtypeStruct((rows, cols, channels), bf16),
+        out_shape=jax.ShapeDtypeStruct((cols, rows, channels), bf16),
         in_specs=[pl.BlockSpec(memory_space=pltpu.VMEM)] * 6,
         out_specs=pl.BlockSpec(memory_space=pltpu.VMEM),
         scratch_shapes=[
-            pltpu.VMEM((rows * pitch, channels), f32),
             pltpu.VMEM((n_col, n_j * width, channels), f32),
             pltpu.VMEM((n_j * width // channels, n_i * width, channels), f32),
-            parcel, parcel, parcel, parcel,
+            parcel, parcel, back, back,
             pltpu.SemaphoreType.DMA((4, n_dev)),
             pltpu.SemaphoreType.DMA((4, n_dev)),
         ],
@@ -303,7 +303,7 @@
     n_row, n_col = mesh.shape["row"], mesh.shape["col"]
     n_dev = n_row * n_col
 
-    def local(pair_rep, *others):
+    def local(pair_rep, pair_mask, *others):
         rows, cols, channels = pair_rep.shape
         by_channel = (
             channels == 128
@@ -315,8 +315,10 @@
             and n_col * cols * (channels // n_dev) % channels == 0
         )
         if by_channel:
-            return make_kernel(n_row, n_col, rows, cols, channels)(pair_rep, *others)
-        return shards(pair_rep, *others)
+            kernel = make_kernel(n_row, n_col, rows, cols, channels)
+            result = kernel(jnp.transpose(pair_rep, (1, 0, 2)), pair_mask.T, *others)
+            return jnp.transpose(result, (1, 0, 2))
+        return shards(pair_rep, pair_mask, *others)
 
     in_specs = (P("row", "col", None), P("row", "col"), P(), P(), P(), P())
     out_specs = P("row", "col", None)

time: 45.7 us -> 41.2 us (0.902)
  local copies, waits for them, and re-layouts: 4.44 us -> 1.52 us
  Pallas kernels: 41 us -> 39.5 us
    pallas_call x1 -> x0, local copies, waits for them, and re-layouts: 1.55 us -> none  [local(): return make_kernel(n_row, n_col, rows, cols, channels)(pair_rep, *others)]
    pallas_call x1, Pallas kernels: 41 us -> 39.5 us  [local(): result = kernel(jnp.transpose(pair_rep, (1, 0, 2)), pair_mask.T, *others)]
    unnamed x2 -> x1, local copies, waits for them, and re-layouts: 2.89 us -> 1.52 us
where the time goes in v2:
time: 41.2 us; the launch traced here: 41.1 us
  Pallas kernels  39.5 us (96%)
  local copies, waits for them, and re-layouts  1.52 us (4%)
    pallas_call x1, Pallas kernels, local(): result = kernel(jnp.transpose(pair_rep, (1, 0, 2)), pair_mask.T, *others)  39.5 us
    unnamed x1, local copies, waits for them, and re-layouts  1.52 us

profile of v2, /device:TPU:0, one launch (start us, length us, event | category | flops | bytes accessed | tf_op | source)
XLA Modules:
  0.0 41.1 jit_solution(17237334462825871239)
XLA Ops:
  0.0 39.5 %shard_map.64 = bf16[12,24,128]{2,1,0:T(8,128)(2,1)} custom-call(bf16[12,24,128]{2,1,0:T(8,128)(2,1)} %bitcast.4, s32[12,24]{1,0:T(8,128)} %bitcast.5, bf16[2,5,128,128]{3,2,1,0:T(8,128)(2,1)} %proj_ref.1, bf16[2,128,128]{2,1,0:T(8,128)(2,1)} %out_w_ref.1, f32[2,2,128]{2,1,0:T(2,128)} %gain_ref.1, f32[2,2,128]{2,1,0:T(2,128)} %bias_ref.1), custom_call_target="tpu_custom_call" | custom-call | tf_op jit(solution)/shard_map/pallas_call | solution.py:319
  39.5 1.5 %copy.8 = bf16[24,12,128]{2,0,1:T(8,128)(2,1)} copy(bf16[24,12,128]{2,0,1:T(8,128)(2,1)} %bitcast.3) | data formatting | bytes 147456
